TPU v7x, 32 devices: a whole 2x2x4 slice. The times are simulated.
32 devices in a mesh: node: 8 (over z, x), feat: 4 (over y, core).
Axes of the slice: x: 2, y: 2, z: 4, core: 2. Of those that a mesh axis runs over, the one named last changes fastest.
Arguments:
- features: bfloat16 [100, 8192], P('feat', 'node'), may hold values from -6 to 6
- edges_one: int32 [1024, 8192], P(None, 'node'), may hold values from 0 to 1, as said below
- w1_self: bfloat16 [100, 256], P('feat'), may hold values from -0.625 to 0.625
- w1_nbr: bfloat16 [100, 256], P('feat'), may hold values from -1.25 to 1.25
- need_blocks: int32 [8, 4], P('node'), may hold values from 0 to 7, as said below
- live_slots: int32 [8, 4], P('node'), may hold values from 0 to 1, as said below
- edges_two: int32 [4096, 8192], P(None, 'node'), may hold values from 0 to 1, as said below
- w2_self: bfloat16 [256, 47], P('feat'), may hold values from -0.375 to 0.375
- w2_nbr: bfloat16 [256, 47], P('feat'), may hold values from -0.5 to 0.5
- labels: int32 [8192], P('node'), may hold values from 0 to 46
Outputs:
- node_loss: float32 [8192], P('node')
- mean_loss: float32 [], replicated
Inputs may be any that keep to these rules, and one draw needn't show every extreme that they name: `need_blocks`: row b holds 4 different blocks; its first entry is b, its second is b plus half the number of blocks, its third is b minus 1, and its entry k is b plus an offset that depends on k alone, modulo the number of blocks. `live_slots`: the first three entries of each row are 1. `edges_one`: each column has exactly 25 ones. `edges_two`: each column t has exactly 10 ones, all in rows of slots that live_slots marks as used for t's block.
All inputs are finite; a program needn't handle non-finite values.
Results may differ from a plain program's by a relative error of at most 0.00065.
Values may be sent and summed in bfloat16 or wider, within the bound.
A program may use at most 128 MiB of HBM per device.

v0:
```python
import jax
import jax.numpy as jnp
from jax import lax
from jax.sharding import PartitionSpec as P

FAN1 = 25
FAN2 = 10


def from_behind(value, axis, steps):
    count = lax.axis_size(axis)
    pairs = [(source, (source + steps) % count) for source in range(count)]
    return lax.ppermute(value, axis, pairs)


def contract(weight, values):
    return lax.dot_general(
        weight, values, (((0,), (0,)), ((), ())), preferred_element_type=jnp.float32
    )


def contract_exact(weight, values):
    return lax.dot_general(
        weight,
        values,
        (((0,), (0,)), ((), ())),
        precision=lax.Precision.HIGHEST,
        preferred_element_type=jnp.float32,
    )


def fetch_offset(hidden, offset):
    nodes = lax.axis_size("node")
    levels = nodes.bit_length() - 1
    carried = hidden
    for level_bit in range(levels):
        moved = from_behind(carried, "node", nodes - (1 << level_bit))
        carried = jnp.where(offset // (1 << level_bit) % 2 == 1, moved, carried)
    return carried


def local(
    features,
    edges_one,
    w1_self,
    w1_nbr,
    need_blocks,
    live_slots,
    edges_two,
    w2_self,
    w2_nbr,
    labels,
):
    block_len = features.shape[1]
    classes = w2_self.shape[1]
    adjacency = edges_one.astype(jnp.bfloat16)
    neighbour = (jnp.dot(features, adjacency, preferred_element_type=jnp.float32) / FAN1).astype(
        jnp.bfloat16
    )
    before = lax.psum_scatter(
        contract(w1_self, features) + contract(w1_nbr, neighbour),
        "feat",
        scatter_dimension=0,
        tiled=True,
    )
    hidden = jax.nn.relu(before).astype(jnp.bfloat16)
    need_row = need_blocks[0]
    live_row = live_slots[0]
    self_term = contract(w2_self, hidden)
    nodes = lax.axis_size("node")
    mine_index = lax.axis_index("node")
    first_rows = edges_two[0:block_len].astype(jnp.bfloat16)
    gathered = jnp.dot(hidden, first_rows, preferred_element_type=jnp.float32)
    for slot in range(1, need_row.shape[0]):
        offset = (need_row[slot] - mine_index + nodes) % nodes
        sources = fetch_offset(hidden, offset)
        rows = edges_two[slot * block_len : (slot + 1) * block_len].astype(jnp.bfloat16)
        term = jnp.dot(sources, rows, preferred_element_type=jnp.float32)
        gathered = gathered + jnp.where(live_row[slot] == 1, term, 0.0)
    neighbour_term = contract_exact(w2_nbr.astype(jnp.float32), gathered)
    logits = lax.psum(self_term + neighbour_term / FAN2, "feat")
    class_ids = jnp.arange(classes, dtype=jnp.int32)[:, None]
    picked = jnp.sum(jnp.where(class_ids == labels[None, :], logits, 0.0), 0)
    node_loss = jnp.log(jnp.sum(jnp.exp(logits), 0)) - picked
    summed = lax.psum(jnp.sum(node_loss), "node")
    mean_loss = summed / (block_len * lax.axis_size("node"))
    return (node_loss, mean_loss)


def solution(mesh):
    return jax.shard_map(
        local,
        mesh=mesh,
        in_specs=(
            P("feat", "node"),
            P(None, "node"),
            P("feat", None),
            P("feat", None),
            P("node", None),
            P("node", None),
            P(None, "node"),
            P("feat", None),
            P("feat", None),
            P("node"),
        ),
        out_specs=(P("node"), P()),
        check_vma=False,
    )
```

profile of v0, /device:TPU:0, one launch (start us, length us, event | category | flops | bytes accessed | tf_op | source)
XLA Modules:
  0.0 156.6 jit_solution(11803071579191022002)
XLA Ops:
  7.2 0.0 reduce-scatter.2.cloned.1.call-start
  7.2 0.8 copy-done
  8.0 1.0 fusion.49
  9.0 3.8 %fusion.10 = f32[256,1024]{1,0:T(8,128)} fusion(f32[256,1024]{1,0:T(8,128)S(1)} %fusion.49, bf16[25,256]{1,0:T(8,128)(2,1)} %param.13, bf16[25,1024]{1,0:T(8,128)(2,1)S(1)} %copy-done, s32[1024,1024]{1,0:T(8,128)} %param.11), kind=kOutput, calls=%fused_computation.11 | convolution fusion | flops 66897920 | bytes 6355456 | tf_op jit(solution)/shard_map/dot_general | solution.py:17
  12.9 0.0 reduce-scatter.2.cloned.1.call-update
  12.9 0.0 all-reduce.2.cloned.1.call-start
  13.0 27.6 %reduce-scatter.2.cloned.1.call-done = f32[64,1024]{1,0:T(8,128)} async-done(((f32[256,1024]{1,0:T(8,128)}), f32[64,1024]{1,0:T(8,128)}) %reduce-scatter.2.cloned.1.call-update) | async-done | bytes 262160 | tf_op jit(solution)/shard_map/reduce_scatter | solution.py:60
  40.6 1.0 maximum_convert_fusion
  41.5 4.3 %collective-permute-start = (bf16[64,1024]{1,0:T(8,128)(2,1)S(1)}, bf16[64,1024]{1,0:T(8,128)(2,1)S(1)}, u32[]{:S(2)}, u32[]{:S(2)}) collective-permute-start(bf16[64,1024]{1,0:T(8,128)(2,1)S(1)} %maximum_convert_fusion), channel_id=1, source_target_pairs={{0,28},{4,0},{8,4},{12,8},{16,12},{20,16},{24,20},{28,24},{1,29},{... | collective-permute-start | bytes 393224 | tf_op jit(solution)/shard_map/ppermute | solution.py:13
  45.8 0.6 fusion.48
  48.6 9.7 %convert.6 = bf16[4096,1024]{1,0:T(8,128)(2,1)} convert(s32[4096,1024]{1,0:T(8,128)} %param.16) | non-fusion elementwise | flops 4194304 | bytes 25165824 | tf_op jit(solution)/shard_map/convert.3
  58.3 0.6 fusion.47
  60.8 0.6 collective-permute-start.1
  61.4 2.1 %fusion.6 = f32[64,1024]{1,0:T(8,128)S(1)} fusion(bf16[64,1024]{1,0:T(8,128)(2,1)S(1)} %maximum_convert_fusion, bf16[4096,1024]{1,0:T(8,128)(2,1)} %convert.6), kind=kOutput, calls=%fused_computation.6 | convolution fusion | flops 134217728 | bytes 2490368 | tf_op jit(solution)/shard_map/dot_general | solution.py:73
  63.4 0.6 collective-permute-start.3
  64.0 0.5 collective-permute-start.5
  64.5 1.8 %collective-permute-done.1 = bf16[64,1024]{1,0:T(8,128)(2,1)S(1)} collective-permute-done((bf16[64,1024]{1,0:T(8,128)(2,1)S(1)}, bf16[64,1024]{1,0:T(8,128)(2,1)S(1)}, u32[]{:S(2)}, u32[]{:S(2)}) %collective-permute-start.1) | collective-permute-done | bytes 131104 | tf_op jit(solution)/shard_map/ppermute | solution.py:13
  66.4 0.6 collective-permute-start.2
  67.1 2.8 %collective-permute-done.3 = bf16[64,1024]{1,0:T(8,128)(2,1)S(1)} collective-permute-done((bf16[64,1024]{1,0:T(8,128)(2,1)S(1)}, bf16[64,1024]{1,0:T(8,128)(2,1)S(1)}, u32[]{:S(2)}, u32[]{:S(2)}) %collective-permute-start.3) | collective-permute-done | bytes 131104 | tf_op jit(solution)/shard_map/ppermute | solution.py:13
  69.9 2.2 %collective-permute-start.4 = (bf16[64,1024]{1,0:T(8,128)(2,1)S(1)}, bf16[64,1024]{1,0:T(8,128)(2,1)S(1)}, u32[]{:S(2)}, u32[]{:S(2)}) collective-permute-start(bf16[64,1024]{1,0:T(8,128)(2,1)S(1)} %broadcast_select_fusion.3), channel_id=1, source_target_pairs={{0,16},{4,20},{8,24},{12,28},{16,0},{20,4},{24,8},{28,12},{1,17},{... | collective-permute-start | bytes 393224 | tf_op jit(solution)/shard_map/ppermute | solution.py:13
  72.1 6.8 %collective-permute-start.6 = (bf16[64,1024]{1,0:T(8,128)(2,1)S(1)}, bf16[64,1024]{1,0:T(8,128)(2,1)S(1)}, u32[]{:S(2)}, u32[]{:S(2)}) collective-permute-start(bf16[64,1024]{1,0:T(8,128)(2,1)S(1)} %broadcast_select_fusion.1), channel_id=1, source_target_pairs={{0,16},{4,20},{8,24},{12,28},{16,0},{20,4},{24,8},{28,12},{1,17},{... | collective-permute-start | bytes 393224 | tf_op jit(solution)/shard_map/ppermute | solution.py:13
  78.8 8.3 %collective-permute-done.4 = bf16[64,1024]{1,0:T(8,128)(2,1)S(1)} collective-permute-done((bf16[64,1024]{1,0:T(8,128)(2,1)S(1)}, bf16[64,1024]{1,0:T(8,128)(2,1)S(1)}, u32[]{:S(2)}, u32[]{:S(2)}) %collective-permute-start.4) | collective-permute-done | bytes 131104 | tf_op jit(solution)/shard_map/ppermute | solution.py:13
  87.2 2.1 %fusion.20 = f32[64,1024]{1,0:T(8,128)S(1)} fusion(bf16[4096,1024]{1,0:T(8,128)(2,1)} %convert.6, bf16[64,1024]{1,0:T(8,128)(2,1)S(1)} %collective-permute-done.4, bf16[64,1024]{1,0:T(8,128)(2,1)S(1)} %broadcast_select_fusion.3, pred[]{:T(512)S(6)} %eq.78, pred[]{:T(512)} %bitcast.3), kind=kOutput, calls=%fused_computation.15 | convolution fusion | flops 134348800 | bytes 2621953 | tf_op jit(solution)/shard_map/dot_general | solution.py:78
  89.3 2.1 %fusion.23 = f32[64,1024]{1,0:T(8,128)S(1)} fusion(bf16[4096,1024]{1,0:T(8,128)(2,1)} %convert.6, bf16[64,1024]{1,0:T(8,128)(2,1)S(1)} %collective-permute-done.6, bf16[64,1024]{1,0:T(8,128)(2,1)S(1)} %broadcast_select_fusion.1, pred[]{:T(512)S(6)} %eq.83, pred[]{:T(512)} %bitcast.5), kind=kOutput, calls=%fused_computation.16 | convolution fusion | flops 134348800 | bytes 2621953 | tf_op jit(solution)/shard_map/dot_general | solution.py:78
  91.4 2.1 %fusion.26 = f32[64,1024]{1,0:T(8,128)S(1)} fusion(f32[64,1024]{1,0:T(8,128)S(1)} %fusion.23, f32[64,1024]{1,0:T(8,128)S(1)} %fusion.20, f32[64,1024]{1,0:T(8,128)S(1)} %fusion.6, bf16[4096,1024]{1,0:T(8,128)(2,1)} %convert.6, bf16[64,1024]{1,0:T(8,128)(2,1)S(1)} %collective-permute-done.2, bf16[64,1024]{1,0:T(8,128)(2,1)S(1)} %broadcast_select_fusion.5, ...), kind=kOutput, calls=%fused_computation.17 | convolution fusion | flops 134545408 | bytes 3408385 | tf_op jit(solution)/shard_map/dot_general | solution.py:78
  93.5 0.3 convolution_multiply_fusion
  93.8 0.8 fusion.29
  94.6 0.0 all-reduce.2.cloned.1.call-update
  94.6 29.2 %all-reduce.2.cloned.1.call-done = f32[47,1024]{1,0:T(8,128)} async-done(((f32[47,1024]{1,0:T(8,128)}), f32[47,1024]{1,0:T(8,128)}) %all-reduce.2.cloned.1.call-update) | async-done | bytes 192528 | tf_op jit(solution)/shard_map/psum | solution.py:81
  123.9 1.0 exponential_reduce_fusion
  124.8 1.2 fusion.46
  126.0 22.0 %psum.15 = f32[]{:T(128)} all-reduce(f32[]{:T(128)} %get-tuple-element.4), channel_id=1, replica_groups=mesh['node'=8,'feat'=4] {'node'}, use_global_device_ids=true, to_apply=%region_5.6 | all-reduce | flops 1 | bytes 8 | tf_op jit(solution)/shard_map/psum | solution.py:85
  (21 shorter events, 0.1 us)
Async XLA Ops:
  7.2 0.8 copy-start
  7.2 38.7 %copy-start.4 = (s32[1,4]{1,0:T(1,128)S(1)}, s32[1,4]{1,0:T(1,128)}, u32[]{:S(2)}) copy-start(s32[1,4]{1,0:T(1,128)} %param.14) | copy-start | bytes 52
  7.2 33.4 %reduce-scatter.2.cloned.1.call-start = ((), (), s32[]{:S(2)}) async-start(), calls=%async_computation.1 | async-start | bytes 1310720 | tf_op jit(solution)/shard_map/reduce_scatter | solution.py:60
  12.9 110.9 %all-reduce.2.cloned.1.call-start = ((), (), s32[]{:S(2)}) async-start(), calls=%async_computation.2 | async-start | bytes 393216 | tf_op jit(solution)/shard_map/psum | solution.py:81
  41.5 19.2 %collective-permute-start = (bf16[64,1024]{1,0:T(8,128)(2,1)S(1)}, bf16[64,1024]{1,0:T(8,128)(2,1)S(1)}, u32[]{:S(2)}, u32[]{:S(2)}) collective-permute-start(bf16[64,1024]{1,0:T(8,128)(2,1)S(1)} %maximum_convert_fusion), channel_id=1, source_target_pairs={{0,28},{4,0},{8,4},{12,8},{16,12},{20,16},{24,20},{28,24},{1,29},{... | collective-permute-start | bytes 393224 | tf_op jit(solution)/shard_map/ppermute | solution.py:13
  48.5 9.7 %copy-start.5 = (s32[1,4]{1,0:T(1,128)S(1)}, s32[1,4]{1,0:T(1,128)}, u32[]{:S(2)}) copy-start(s32[1,4]{1,0:T(1,128)} %param.15) | copy-start | bytes 52
  48.6 12.2 %copy-start.1 = (f32[64,1024]{1,0:T(8,128)S(1)}, f32[64,1024]{1,0:T(8,128)}, u32[]{:S(2)}) copy-start(f32[64,1024]{1,0:T(8,128)} %reduce-scatter.2.cloned.1.call-done) | copy-start | bytes 786436
  60.8 5.6 %collective-permute-start.1 = (bf16[64,1024]{1,0:T(8,128)(2,1)S(1)}, bf16[64,1024]{1,0:T(8,128)(2,1)S(1)}, u32[]{:S(2)}, u32[]{:S(2)}) collective-permute-start(bf16[64,1024]{1,0:T(8,128)(2,1)S(1)} %get-tuple-element.6), channel_id=1, source_target_pairs={{0,24},{4,28},{8,0},{12,4},{16,8},{20,12},{24,16},{28,20},{1,25},{... | collective-permute-start | bytes 393224 | tf_op jit(solution)/shard_map/ppermute | solution.py:13
  63.4 6.4 %collective-permute-start.3 = (bf16[64,1024]{1,0:T(8,128)(2,1)S(1)}, bf16[64,1024]{1,0:T(8,128)(2,1)S(1)}, u32[]{:S(2)}, u32[]{:S(2)}) collective-permute-start(bf16[64,1024]{1,0:T(8,128)(2,1)S(1)} %get-tuple-element.8), channel_id=1, source_target_pairs={{0,24},{4,28},{8,0},{12,4},{16,8},{20,12},{24,16},{28,20},{1,25},{... | collective-permute-start | bytes 393224 | tf_op jit(solution)/shard_map/ppermute | solution.py:13
  64.0 8.0 %collective-permute-start.5 = (bf16[64,1024]{1,0:T(8,128)(2,1)S(1)}, bf16[64,1024]{1,0:T(8,128)(2,1)S(1)}, u32[]{:S(2)}, u32[]{:S(2)}) collective-permute-start(bf16[64,1024]{1,0:T(8,128)(2,1)S(1)} %get-tuple-element.7), channel_id=1, source_target_pairs={{0,24},{4,28},{8,0},{12,4},{16,8},{20,12},{24,16},{28,20},{1,25},{... | collective-permute-start | bytes 393224 | tf_op jit(solution)/shard_map/ppermute | solution.py:13
  66.4 25.0 %collective-permute-start.2 = (bf16[64,1024]{1,0:T(8,128)(2,1)S(1)}, bf16[64,1024]{1,0:T(8,128)(2,1)S(1)}, u32[]{:S(2)}, u32[]{:S(2)}) collective-permute-start(bf16[64,1024]{1,0:T(8,128)(2,1)S(1)} %broadcast_select_fusion.5), channel_id=1, source_target_pairs={{0,16},{4,20},{8,24},{12,28},{16,0},{20,4},{24,8},{28,12},{1,17},{... | collective-permute-start | bytes 393224 | tf_op jit(solution)/shard_map/ppermute | solution.py:13
  69.9 17.3 %collective-permute-start.4 = (bf16[64,1024]{1,0:T(8,128)(2,1)S(1)}, bf16[64,1024]{1,0:T(8,128)(2,1)S(1)}, u32[]{:S(2)}, u32[]{:S(2)}) collective-permute-start(bf16[64,1024]{1,0:T(8,128)(2,1)S(1)} %broadcast_select_fusion.3), channel_id=1, source_target_pairs={{0,16},{4,20},{8,24},{12,28},{16,0},{20,4},{24,8},{28,12},{1,17},{... | collective-permute-start | bytes 393224 | tf_op jit(solution)/shard_map/ppermute | solution.py:13
  72.1 17.2 %collective-permute-start.6 = (bf16[64,1024]{1,0:T(8,128)(2,1)S(1)}, bf16[64,1024]{1,0:T(8,128)(2,1)S(1)}, u32[]{:S(2)}, u32[]{:S(2)}) collective-permute-start(bf16[64,1024]{1,0:T(8,128)(2,1)S(1)} %broadcast_select_fusion.1), channel_id=1, source_target_pairs={{0,16},{4,20},{8,24},{12,28},{16,0},{20,4},{24,8},{28,12},{1,17},{... | collective-permute-start | bytes 393224 | tf_op jit(solution)/shard_map/ppermute | solution.py:13
  87.2 6.3 %copy-start.2 = (bf16[64,47]{0,1:T(8,128)(2,1)S(1)}, bf16[64,47]{0,1:T(8,128)(2,1)}, u32[]{:S(2)}) copy-start(bf16[64,47]{0,1:T(8,128)(2,1)} %param.18) | copy-start | bytes 18052
  87.2 6.6 %copy-start.3 = (bf16[64,47]{0,1:T(8,128)(2,1)S(1)}, bf16[64,47]{0,1:T(8,128)(2,1)}, u32[]{:S(2)}) copy-start(bf16[64,47]{0,1:T(8,128)(2,1)} %param.17) | copy-start | bytes 18052
  89.3 34.6 %copy-start.6 = (s32[1024]{0:T(1024)S(1)}, s32[1024]{0:T(1024)}, u32[]{:S(2)}) copy-start(s32[1024]{0:T(1024)} %param.19) | copy-start | bytes 12292
Sparse Core Ops, SparseCore 0:
  13.0 27.4 reduce-scatter.1
  94.7 29.0 all-reduce.1
where the time goes:
time: 157 us
  waiting for transfers between devices  69.8 us (44%)
  blocking collectives  22 us (14%)
  between operations  20 us (13%)
  starting transfers between devices  15.7 us (10%)
  matrix products  14.3 us (9%)
  other arithmetic  12.9 us (8%)
  local copies, waits for them, and re-layouts  1.99 us (1%)
    psum x1, waiting for transfers between devices, local(): logits = lax.psum(self_term + neighbour_term / FAN2, 'feat')  29.2 us
    reduce_scatter x1, waiting for transfers between devices, local(): lax.psum_scatter(contract(w1_self, features) + contract(w1_nbr, neighbour...  27.6 us
    psum x1, blocking collectives, local(): summed = lax.psum(jnp.sum(node_loss), 'node')  22 us
    ppermute x7, starting transfers between devices, from_behind(): return lax.ppermute(value, axis, pairs)  15.6 us
    ppermute x7, waiting for transfers between devices, from_behind(): return lax.ppermute(value, axis, pairs)  13 us
    another operation x1, other arithmetic  9.68 us
    dot_general x3, matrix products, local(): term = jnp.dot(sources, rows, preferred_element_type=jnp.float32)  6.26 us
    dot_general x3, matrix products, contract(): lax.dot_general(weight, values, (((0,), (0,)), ((), ())), preferred_eleme...  5.7 us
  transfers between devices with their start and end apart: 9, of which 5 were waited for; matrix products, arithmetic and copies ran while one was open for 11% of the time, Pallas kernels for 0%

commit v1 on v0

--- a/solution.py
+++ b/solution.py
@@ -78,7 +78,7 @@
         term = jnp.dot(sources, rows, preferred_element_type=jnp.float32)
         gathered = gathered + jnp.where(live_row[slot] == 1, term, 0.0)
     neighbour_term = contract_exact(w2_nbr.astype(jnp.float32), gathered)
-    logits = lax.psum(self_term + neighbour_term / FAN2, "feat")
+    logits = jnp.sum(lax.all_gather(self_term + neighbour_term / FAN2, "feat"), axis=0)
     class_ids = jnp.arange(classes, dtype=jnp.int32)[:, None]
     picked = jnp.sum(jnp.where(class_ids == labels[None, :], logits, 0.0), 0)
     node_loss = jnp.log(jnp.sum(jnp.exp(logits), 0)) - picked

time: 157 us -> 132 us (0.84)
  waiting for transfers between devices: 69.8 us -> 40.6 us
  blocking collectives: 22 us -> 27.4 us
    psum x1 -> x0, waiting for transfers between devices: 29.2 us -> none  [local(): logits = lax.psum(self_term + neighbour_term / FAN2, 'feat')]
    all_gather x0 -> x1, blocking collectives: none -> 7.67 us  [local(): lax.all_gather(self_term + neighbour_term / FAN2, 'feat')]
    psum x1, blocking collectives: 22 us -> 19.8 us  [local(): summed = lax.psum(jnp.sum(node_loss), 'node')]
  transfers between devices with their start and end apart: 9 -> 8, of which waited for: 5 -> 4; matrix products, arithmetic and copies ran while one was open for 11% -> 13% of each run, Pallas kernels for 0% -> 0%
where the time goes in v1:
time: 132 us
  waiting for transfers between devices  40.6 us (31%)
  blocking collectives  27.4 us (21%)
  between operations  20.2 us (15%)
  starting transfers between devices  15.6 us (12%)
  matrix products  13.6 us (10%)
  other arithmetic  12 us (9%)
  local copies, waits for them, and re-layouts  2.06 us (2%)
    reduce_scatter x1, waiting for transfers between devices, local(): lax.psum_scatter(contract(w1_self, features) + contract(w1_nbr, neighbour...  27.7 us
    psum x1, blocking collectives, local(): summed = lax.psum(jnp.sum(node_loss), 'node')  19.8 us
    ppermute x7, starting transfers between devices, from_behind(): return lax.ppermute(value, axis, pairs)  15.6 us
    ppermute x7, waiting for transfers between devices, from_behind(): return lax.ppermute(value, axis, pairs)  13 us
    another operation x1, other arithmetic  9.66 us
    all_gather x1, blocking collectives, local(): lax.all_gather(self_term + neighbour_term / FAN2, 'feat')  7.67 us
    dot_general x3, matrix products, local(): term = jnp.dot(sources, rows, preferred_element_type=jnp.float32)  6.26 us
    dot_general x3, matrix products, contract(): lax.dot_general(weight, values, (((0,), (0,)), ((), ())), preferred_eleme...  5.03 us
  transfers between devices with their start and end apart: 8, of which 4 were waited for; matrix products, arithmetic and copies ran while one was open for 13% of the time, Pallas kernels for 0%

profile of v1, /device:TPU:0, one launch (start us, length us, event | category | flops | bytes accessed | tf_op | source)
XLA Modules:
  0.0 131.5 jit_solution(10531280238830266225)
XLA Ops:
  7.2 0.0 copy-start
  7.2 0.0 reduce-scatter.2.cloned.1.call-start
  7.2 0.8 copy-done
  8.0 1.0 fusion.49
  9.0 3.8 %fusion.10 = f32[256,1024]{1,0:T(8,128)} fusion(f32[256,1024]{1,0:T(8,128)S(1)} %fusion.49, bf16[25,256]{1,0:T(8,128)(2,1)} %param.13, bf16[25,1024]{1,0:T(8,128)(2,1)S(1)} %copy-done, s32[1024,1024]{1,0:T(8,128)} %param.11), kind=kOutput, calls=%fused_computation.11 | convolution fusion | flops 66897920 | bytes 6355456 | tf_op jit(solution)/shard_map/dot_general | solution.py:17
  12.9 0.0 reduce-scatter.2.cloned.1.call-update
  12.9 27.7 %reduce-scatter.2.cloned.1.call-done = f32[64,1024]{1,0:T(8,128)} async-done(((f32[256,1024]{1,0:T(8,128)}), f32[64,1024]{1,0:T(8,128)}) %reduce-scatter.2.cloned.1.call-update) | async-done | bytes 262160 | tf_op jit(solution)/shard_map/reduce_scatter | solution.py:60
  40.6 1.0 maximum_convert_fusion
  41.5 4.3 %collective-permute-start = (bf16[64,1024]{1,0:T(8,128)(2,1)S(1)}, bf16[64,1024]{1,0:T(8,128)(2,1)S(1)}, u32[]{:S(2)}, u32[]{:S(2)}) collective-permute-start(bf16[64,1024]{1,0:T(8,128)(2,1)S(1)} %maximum_convert_fusion), channel_id=1, source_target_pairs={{0,28},{4,0},{8,4},{12,8},{16,12},{20,16},{24,20},{28,24},{1,29},{... | collective-permute-start | bytes 393224 | tf_op jit(solution)/shard_map/ppermute | solution.py:13
  45.8 0.6 fusion.48
  48.6 0.0 copy-start.5
  48.6 9.7 %convert.6 = bf16[4096,1024]{1,0:T(8,128)(2,1)} convert(s32[4096,1024]{1,0:T(8,128)} %param.16) | non-fusion elementwise | flops 4194304 | bytes 25165824 | tf_op jit(solution)/shard_map/convert.3
  58.3 0.7 fusion.47
  61.0 0.6 collective-permute-start.1
  61.6 2.1 %fusion.6 = f32[64,1024]{1,0:T(8,128)S(1)} fusion(bf16[64,1024]{1,0:T(8,128)(2,1)S(1)} %maximum_convert_fusion, bf16[4096,1024]{1,0:T(8,128)(2,1)} %convert.6), kind=kOutput, calls=%fused_computation.6 | convolution fusion | flops 134217728 | bytes 2490368 | tf_op jit(solution)/shard_map/dot_general | solution.py:73
  63.6 0.6 collective-permute-start.3
  64.2 0.5 collective-permute-start.5
  64.8 1.8 %collective-permute-done.1 = bf16[64,1024]{1,0:T(8,128)(2,1)S(1)} collective-permute-done((bf16[64,1024]{1,0:T(8,128)(2,1)S(1)}, bf16[64,1024]{1,0:T(8,128)(2,1)S(1)}, u32[]{:S(2)}, u32[]{:S(2)}) %collective-permute-start.1) | collective-permute-done | bytes 131104 | tf_op jit(solution)/shard_map/ppermute | solution.py:13
  66.6 0.6 collective-permute-start.2
  67.3 2.8 %collective-permute-done.3 = bf16[64,1024]{1,0:T(8,128)(2,1)S(1)} collective-permute-done((bf16[64,1024]{1,0:T(8,128)(2,1)S(1)}, bf16[64,1024]{1,0:T(8,128)(2,1)S(1)}, u32[]{:S(2)}, u32[]{:S(2)}) %collective-permute-start.3) | collective-permute-done | bytes 131104 | tf_op jit(solution)/shard_map/ppermute | solution.py:13
  70.1 2.2 %collective-permute-start.4 = (bf16[64,1024]{1,0:T(8,128)(2,1)S(1)}, bf16[64,1024]{1,0:T(8,128)(2,1)S(1)}, u32[]{:S(2)}, u32[]{:S(2)}) collective-permute-start(bf16[64,1024]{1,0:T(8,128)(2,1)S(1)} %broadcast_select_fusion.3), channel_id=1, source_target_pairs={{0,16},{4,20},{8,24},{12,28},{16,0},{20,4},{24,8},{28,12},{1,17},{... | collective-permute-start | bytes 393224 | tf_op jit(solution)/shard_map/ppermute | solution.py:13
  72.3 6.8 %collective-permute-start.6 = (bf16[64,1024]{1,0:T(8,128)(2,1)S(1)}, bf16[64,1024]{1,0:T(8,128)(2,1)S(1)}, u32[]{:S(2)}, u32[]{:S(2)}) collective-permute-start(bf16[64,1024]{1,0:T(8,128)(2,1)S(1)} %broadcast_select_fusion.1), channel_id=1, source_target_pairs={{0,16},{4,20},{8,24},{12,28},{16,0},{20,4},{24,8},{28,12},{1,17},{... | collective-permute-start | bytes 393224 | tf_op jit(solution)/shard_map/ppermute | solution.py:13
  79.0 8.3 %collective-permute-done.4 = bf16[64,1024]{1,0:T(8,128)(2,1)S(1)} collective-permute-done((bf16[64,1024]{1,0:T(8,128)(2,1)S(1)}, bf16[64,1024]{1,0:T(8,128)(2,1)S(1)}, u32[]{:S(2)}, u32[]{:S(2)}) %collective-permute-start.4) | collective-permute-done | bytes 131104 | tf_op jit(solution)/shard_map/ppermute | solution.py:13
  87.4 2.1 %fusion.20 = f32[64,1024]{1,0:T(8,128)S(1)} fusion(bf16[4096,1024]{1,0:T(8,128)(2,1)} %convert.6, bf16[64,1024]{1,0:T(8,128)(2,1)S(1)} %collective-permute-done.4, bf16[64,1024]{1,0:T(8,128)(2,1)S(1)} %broadcast_select_fusion.3, pred[]{:T(512)S(6)} %eq.78, pred[]{:T(512)} %bitcast.3), kind=kOutput, calls=%fused_computation.15 | convolution fusion | flops 134348800 | bytes 2621953 | tf_op jit(solution)/shard_map/dot_general | solution.py:78
  89.5 2.1 %fusion.23 = f32[64,1024]{1,0:T(8,128)S(1)} fusion(bf16[4096,1024]{1,0:T(8,128)(2,1)} %convert.6, bf16[64,1024]{1,0:T(8,128)(2,1)S(1)} %collective-permute-done.6, bf16[64,1024]{1,0:T(8,128)(2,1)S(1)} %broadcast_select_fusion.1, pred[]{:T(512)S(6)} %eq.83, pred[]{:T(512)} %bitcast.5), kind=kOutput, calls=%fused_computation.16 | convolution fusion | flops 134348800 | bytes 2621953 | tf_op jit(solution)/shard_map/dot_general | solution.py:78
  91.6 2.1 %fusion.26 = f32[64,1024]{1,0:T(8,128)S(1)} fusion(f32[64,1024]{1,0:T(8,128)S(1)} %fusion.23, f32[64,1024]{1,0:T(8,128)S(1)} %fusion.20, f32[64,1024]{1,0:T(8,128)S(1)} %fusion.6, bf16[4096,1024]{1,0:T(8,128)(2,1)} %convert.6, bf16[64,1024]{1,0:T(8,128)(2,1)S(1)} %collective-permute-done.2, bf16[64,1024]{1,0:T(8,128)(2,1)S(1)} %broadcast_select_fusion.5, ...), kind=kOutput, calls=%fused_computation.17 | convolution fusion | flops 134545408 | bytes 3408385 | tf_op jit(solution)/shard_map/dot_general | solution.py:78
  93.7 0.3 convolution_multiply_fusion
  94.0 0.2 fusion.29
  94.1 7.7 %all-gather.1 = f32[4,47,1024]{2,1,0:T(8,128)S(1)} all-gather(f32[1,47,1024]{2,1,0:T(8,128)S(1)} %fusion.29), channel_id=2, replica_groups=mesh['node'=8,'feat'=4] {'feat'}, dimensions={0}, use_global_device_ids=true | all-gather | bytes 962560 | tf_op jit(solution)/shard_map/all_gather | solution.py:81
  101.9 0.1 exponential_reduce_fusion
  101.9 1.2 fusion.46
  103.1 19.8 %psum.7 = f32[]{:T(128)} all-reduce(f32[]{:T(128)} %get-tuple-element.4), channel_id=1, replica_groups=mesh['node'=8,'feat'=4] {'node'}, use_global_device_ids=true, to_apply=%region_5.6 | all-reduce | flops 1 | bytes 8 | tf_op jit(solution)/shard_map/psum | solution.py:85
  (20 shorter events, 0.2 us)
Async XLA Ops:
  7.2 0.8 copy-start
  7.2 38.7 %copy-start.4 = (s32[1,4]{1,0:T(1,128)S(1)}, s32[1,4]{1,0:T(1,128)}, u32[]{:S(2)}) copy-start(s32[1,4]{1,0:T(1,128)} %param.14) | copy-start | bytes 52
  7.2 33.4 %reduce-scatter.2.cloned.1.call-start = ((), (), s32[]{:S(2)}) async-start(), calls=%async_computation.1 | async-start | bytes 1310720 | tf_op jit(solution)/shard_map/reduce_scatter | solution.py:60
  41.5 19.4 %collective-permute-start = (bf16[64,1024]{1,0:T(8,128)(2,1)S(1)}, bf16[64,1024]{1,0:T(8,128)(2,1)S(1)}, u32[]{:S(2)}, u32[]{:S(2)}) collective-permute-start(bf16[64,1024]{1,0:T(8,128)(2,1)S(1)} %maximum_convert_fusion), channel_id=1, source_target_pairs={{0,28},{4,0},{8,4},{12,8},{16,12},{20,16},{24,20},{28,24},{1,29},{... | collective-permute-start | bytes 393224 | tf_op jit(solution)/shard_map/ppermute | solution.py:13
  48.6 9.7 %copy-start.5 = (s32[1,4]{1,0:T(1,128)S(1)}, s32[1,4]{1,0:T(1,128)}, u32[]{:S(2)}) copy-start(s32[1,4]{1,0:T(1,128)} %param.15) | copy-start | bytes 52
  48.6 12.3 %copy-start.1 = (f32[64,1024]{1,0:T(8,128)S(1)}, f32[64,1024]{1,0:T(8,128)}, u32[]{:S(2)}) copy-start(f32[64,1024]{1,0:T(8,128)} %reduce-scatter.2.cloned.1.call-done) | copy-start | bytes 786436
  61.0 5.6 %collective-permute-start.1 = (bf16[64,1024]{1,0:T(8,128)(2,1)S(1)}, bf16[64,1024]{1,0:T(8,128)(2,1)S(1)}, u32[]{:S(2)}, u32[]{:S(2)}) collective-permute-start(bf16[64,1024]{1,0:T(8,128)(2,1)S(1)} %get-tuple-element.6), channel_id=1, source_target_pairs={{0,24},{4,28},{8,0},{12,4},{16,8},{20,12},{24,16},{28,20},{1,25},{... | collective-permute-start | bytes 393224 | tf_op jit(solution)/shard_map/ppermute | solution.py:13
  63.6 6.4 %collective-permute-start.3 = (bf16[64,1024]{1,0:T(8,128)(2,1)S(1)}, bf16[64,1024]{1,0:T(8,128)(2,1)S(1)}, u32[]{:S(2)}, u32[]{:S(2)}) collective-permute-start(bf16[64,1024]{1,0:T(8,128)(2,1)S(1)} %get-tuple-element.8), channel_id=1, source_target_pairs={{0,24},{4,28},{8,0},{12,4},{16,8},{20,12},{24,16},{28,20},{1,25},{... | collective-permute-start | bytes 393224 | tf_op jit(solution)/shard_map/ppermute | solution.py:13
  64.2 8.0 %collective-permute-start.5 = (bf16[64,1024]{1,0:T(8,128)(2,1)S(1)}, bf16[64,1024]{1,0:T(8,128)(2,1)S(1)}, u32[]{:S(2)}, u32[]{:S(2)}) collective-permute-start(bf16[64,1024]{1,0:T(8,128)(2,1)S(1)} %get-tuple-element.7), channel_id=1, source_target_pairs={{0,24},{4,28},{8,0},{12,4},{16,8},{20,12},{24,16},{28,20},{1,25},{... | collective-permute-start | bytes 393224 | tf_op jit(solution)/shard_map/ppermute | solution.py:13
  66.6 25.0 %collective-permute-start.2 = (bf16[64,1024]{1,0:T(8,128)(2,1)S(1)}, bf16[64,1024]{1,0:T(8,128)(2,1)S(1)}, u32[]{:S(2)}, u32[]{:S(2)}) collective-permute-start(bf16[64,1024]{1,0:T(8,128)(2,1)S(1)} %broadcast_select_fusion.5), channel_id=1, source_target_pairs={{0,16},{4,20},{8,24},{12,28},{16,0},{20,4},{24,8},{28,12},{1,17},{... | collective-permute-start | bytes 393224 | tf_op jit(solution)/shard_map/ppermute | solution.py:13
  70.1 17.3 %collective-permute-start.4 = (bf16[64,1024]{1,0:T(8,128)(2,1)S(1)}, bf16[64,1024]{1,0:T(8,128)(2,1)S(1)}, u32[]{:S(2)}, u32[]{:S(2)}) collective-permute-start(bf16[64,1024]{1,0:T(8,128)(2,1)S(1)} %broadcast_select_fusion.3), channel_id=1, source_target_pairs={{0,16},{4,20},{8,24},{12,28},{16,0},{20,4},{24,8},{28,12},{1,17},{... | collective-permute-start | bytes 393224 | tf_op jit(solution)/shard_map/ppermute | solution.py:13
  72.3 17.2 %collective-permute-start.6 = (bf16[64,1024]{1,0:T(8,128)(2,1)S(1)}, bf16[64,1024]{1,0:T(8,128)(2,1)S(1)}, u32[]{:S(2)}, u32[]{:S(2)}) collective-permute-start(bf16[64,1024]{1,0:T(8,128)(2,1)S(1)} %broadcast_select_fusion.1), channel_id=1, source_target_pairs={{0,16},{4,20},{8,24},{12,28},{16,0},{20,4},{24,8},{28,12},{1,17},{... | collective-permute-start | bytes 393224 | tf_op jit(solution)/shard_map/ppermute | solution.py:13
  87.4 6.3 %copy-start.2 = (bf16[64,47]{0,1:T(8,128)(2,1)S(1)}, bf16[64,47]{0,1:T(8,128)(2,1)}, u32[]{:S(2)}) copy-start(bf16[64,47]{0,1:T(8,128)(2,1)} %param.18) | copy-start | bytes 18052
  87.4 6.6 %copy-start.3 = (bf16[64,47]{0,1:T(8,128)(2,1)S(1)}, bf16[64,47]{0,1:T(8,128)(2,1)}, u32[]{:S(2)}) copy-start(bf16[64,47]{0,1:T(8,128)(2,1)} %param.17) | copy-start | bytes 18052
  89.5 12.4 %copy-start.6 = (s32[1024]{0:T(1024)S(1)}, s32[1024]{0:T(1024)}, u32[]{:S(2)}) copy-start(s32[1024]{0:T(1024)} %param.19) | copy-start | bytes 12292
Sparse Core Ops, SparseCore 0:
  13.0 27.4 reduce-scatter.1
